TPU v7x, 32 devices: a whole 2x2x4 slice. The times are simulated.
32 devices in a mesh: station: 16 (over z, x, core), chan: 2 (over y).
Axes of the slice: x: 2, y: 2, z: 4, core: 2. Of those that a mesh axis runs over, the one named last changes fastest.
Arguments:
- samples: float32 [2, 16, 256, 128, 256], P(None, 'station', 'chan'), may hold values from -6 to 6
- weights: float32 [2, 16, 32, 256, 256], P(None, 'station', None, 'chan'), may hold values from -6 to 6
- antenna_flags: int32 [16, 256], P('station', 'chan'), may hold values from 0 to 1, as said below
- subband_table: int32 [256], replicated, may hold values from 0 to 255, each once
Outputs:
- visibilities: float32 [256, 2, 16, 32, 16], P('chan', None, 'station')
Inputs may be any that keep to these rules, and one draw needn't show every extreme that they name: `antenna_flags`: every station has at least 32 antennas with flag 1. `subband_table`: a permutation of 0 to 255.
All inputs are finite; a program needn't handle non-finite values.
Results may differ from a plain program's by a relative error of at most 0.0019.
Values may be sent and summed in bfloat16 or wider, within the bound.
A program may use at most 192 MiB of HBM per device.

v0:
```python
import jax
import jax.numpy as jnp
from jax import lax
from jax.sharding import PartitionSpec as P


def beamform(steer, signal):

    def contract(left, right):
        return jnp.einsum(
            "sabf,satf->fsbt",
            left,
            right,
            precision=lax.Precision.HIGHEST,
            preferred_element_type=jnp.float32,
        )

    real_part = contract(steer[0], signal[0]) - contract(steer[1], signal[1])
    imag_part = contract(steer[0], signal[1]) + contract(steer[1], signal[0])
    return jnp.stack([real_part, imag_part], axis=1)


def correlate(stacked, arrived):
    return jnp.einsum("ofcsbt,fcrbt->fosbr", stacked, arrived, preferred_element_type=jnp.float32)


def with_swapped(beam_data):
    swapped = jnp.stack([beam_data[:, 1], -beam_data[:, 0]], axis=1)
    return jnp.stack([beam_data, swapped], axis=0)


def on_device(samples, weights, antenna_flags, subband_table):
    usable = antenna_flags.astype(jnp.float32)
    usable_count = lax.psum(jnp.sum(usable, axis=1), "chan")
    gain_scale = lax.rsqrt(usable_count)
    masked = samples * usable[None, :, :, None, None]
    steer = jnp.swapaxes(weights, 2, 3)
    beam_sum = lax.psum_scatter(
        beamform(jnp.take(steer, subband_table, axis=4), jnp.take(masked, subband_table, axis=4)),
        "chan",
        scatter_dimension=0,
        tiled=True,
    )
    beam_data = (beam_sum * gain_scale[None, None, :, None, None]).astype(jnp.bfloat16)
    stacked = with_swapped(beam_data)
    return correlate(stacked, lax.all_gather(beam_data, "station", axis=2, tiled=True))


def solution(mesh):
    in_specs = (
        P(None, "station", "chan", None, None),
        P(None, "station", None, "chan", None),
        P("station", "chan"),
        P(),
    )
    out_specs = P("chan", None, "station", None, None)
    return jax.shard_map(
        on_device, mesh=mesh, in_specs=in_specs, out_specs=out_specs, check_vma=False
    )
```

profile of v0, /device:TPU:0, one launch (start us, length us, event | category | flops | bytes accessed | tf_op | source)
XLA Modules:
  0.0 543.0 jit_solution(18153403711742747376)
XLA Ops:
  6.5 0.0 reduce-scatter.5.cloned.1.call-start
  6.5 0.7 compare_select_fusion
  7.2 0.7 compare_and_fusion
  7.9 0.0 copy-start.2
  7.9 35.5 %copy.45 = f32[2,1,128,128,256]{3,2,0,4,1:T(8,128)} copy(f32[2,1,128,128,256]{4,3,2,1,0:T(8,128)} %param.4) | data formatting | bytes 67108864 | tf_op args[0]
  43.4 0.0 copy-done.2
  43.4 10.3 %copy.43 = f32[2,1,32,128,256]{3,2,0,4,1:T(8,128)} copy(f32[2,1,32,128,256]{4,3,2,1,0:T(8,128)} %param.5) | data formatting | bytes 16777216 | tf_op args[1]
  53.8 23.7 %multiply_bitcast_fusion = f32[2,128,128,256]{2,1,0,3:T(8,128)} fusion(f32[2,1,128,128,256]{3,2,0,4,1:T(8,128)} %copy.45, f32[128]{0:T(128)S(1)} %convert_bitcast_fusion), kind=kLoop, calls=%fused_computation.5 | loop fusion | flops 8388608 | bytes 67109376 | tf_op jit(solution)/shard_map/mul | solution.py:36
  77.4 23.6 %gather_fusion.1 = f32[256,2,128,128]{3,2,1,0:T(8,128)} fusion(f32[2,128,128,256]{2,1,0,3:T(8,128)} %multiply_bitcast_fusion, s32[1024]{0:T(1024)S(1)} %pad_clamp_fusion), kind=kCustom, calls=%fused_computation.1 | custom fusion | bytes 67109888 | tf_op jit(solution)/shard_map/jit(_take)/gather | solution.py:39
  101.0 7.7 %gather_fusion = f32[256,2,128,32]{2,3,1,0:T(8,128)} fusion(f32[2,128,32,256]{1,2,0,3:T(8,128)} %bitcast.80, s32[1024]{0:T(1024)S(1)} %pad_clamp_fusion), kind=kCustom, calls=%fused_computation | custom fusion | bytes 16778240 | tf_op jit(solution)/shard_map/jit(_take)/gather | solution.py:39
  108.7 12.9 %bitcast_select_fusion = f32[2,1,128,128,256]{3,2,4,1,0:T(8,128)S(1)} fusion(f32[256,2,128,128]{3,2,1,0:T(8,128)} %gather_fusion.1, pred[256]{0:T(512)(128)(4,1)S(1)} %compare_and_fusion), kind=kLoop, calls=%fused_computation.2 | loop fusion | flops 8388608 | bytes 67109120 | tf_op jit(solution)/shard_map/jit(_take)/select_n | solution.py:39
  121.6 6.0 %bitcast_select_fusion.1 = f32[2,1,128,32,256]{2,3,4,1,0:T(8,128)} fusion(f32[256,2,128,32]{2,3,1,0:T(8,128)} %gather_fusion, pred[256]{0:T(512)(128)(4,1)S(1)} %compare_and_fusion), kind=kLoop, calls=%fused_computation.14 | loop fusion | flops 2097152 | bytes 16777472 | tf_op jit(solution)/shard_map/jit(_take)/select_n | solution.py:39
  127.6 17.8 %fusion.3 = f32[256,32,128]{2,1,0:T(8,128)} fusion(f32[2,1,128,128,256]{3,2,4,1,0:T(8,128)S(1)} %bitcast_select_fusion, f32[2,1,128,32,256]{2,3,4,1,0:T(8,128)} %bitcast_select_fusion.1), kind=kOutput, calls=%fused_computation.9 | convolution fusion | flops 1610612736 | bytes 25165824 | tf_op jit(solution)/shard_map/sabf,satf->fsbt/dot_general | solution.py:10
  145.4 18.0 %fusion.2 = f32[256,32,128]{2,1,0:T(8,128)} fusion(f32[2,1,128,128,256]{3,2,4,1,0:T(8,128)S(1)} %bitcast_select_fusion, f32[2,1,128,32,256]{2,3,4,1,0:T(8,128)} %bitcast_select_fusion.1), kind=kOutput, calls=%fused_computation.8 | convolution fusion | flops 1610612736 | bytes 25165824 | tf_op jit(solution)/shard_map/sabf,satf->fsbt/dot_general | solution.py:10
  163.4 18.7 %subtract_bitcast_fusion = f32[256,1,1,32,128]{4,3,0,2,1:T(8,128)} fusion(f32[256,32,128]{2,1,0:T(8,128)} %fusion.3, f32[2,1,128,128,256]{3,2,4,1,0:T(8,128)S(1)} %bitcast_select_fusion, f32[2,1,128,32,256]{2,3,4,1,0:T(8,128)} %bitcast_select_fusion.1), kind=kOutput, calls=%fused_computation.23 | convolution fusion | flops 1611661312 | bytes 29360128 | tf_op jit(solution)/shard_map/sabf,satf->fsbt/dot_general | solution.py:10
  182.0 19.0 %add_bitcast_fusion = f32[256,1,1,32,128]{4,3,0,2,1:T(8,128)} fusion(f32[256,32,128]{2,1,0:T(8,128)} %fusion.2, f32[2,1,128,128,256]{3,2,4,1,0:T(8,128)S(1)} %bitcast_select_fusion, f32[2,1,128,32,256]{2,3,4,1,0:T(8,128)} %bitcast_select_fusion.1), kind=kOutput, calls=%fused_computation.22 | convolution fusion | flops 1611661312 | bytes 29360128 | tf_op jit(solution)/shard_map/sabf,satf->fsbt/dot_general | solution.py:10
  201.1 4.4 pad_maximum_fusion
  205.5 1.4 copy.53
  207.0 10.9 %copy.65 = f32[32,8,64,128]{3,1,2,0:T(8,128)} copy(f32[32,8,64,128]{3,2,1,0:T(8,128)S(1)} %bitcast.81) | data formatting | bytes 16777216
  217.8 0.0 reduce-scatter.5.cloned.1.call-update
  217.9 0.0 all-gather.2.cloned.1.call-start
  217.9 0.6 convert_reduce_fusion
  218.5 6.7 %psum.7 = f32[1]{0:T(128)} all-reduce(f32[1]{0:T(128)} %bitcast.14), channel_id=1, replica_groups=mesh['station'=16,'chan'=2] {'chan'}, use_global_device_ids=true, to_apply=%region_2.3 | all-reduce | flops 1 | bytes 8 | tf_op jit(solution)/shard_map/psum | solution.py:34
  225.9 94.1 %reduce-scatter.5.cloned.1.call-done = f32[128,8192]{1,0:T(8,128)} async-done(((f32[256,8192]{1,0:T(8,128)}), f32[128,8192]{1,0:T(8,128)}) %reduce-scatter.5.cloned.1.call-update) | async-done | bytes 4194320
  320.1 2.9 copy.57
  323.0 0.0 copy-start
  323.0 1.9 copy-done
  324.9 1.9 fusion.8
  326.9 0.0 all-gather.2.cloned.1.call-update
  326.9 0.0 copy-start.1
  326.9 1.9 fusion.13
  328.8 0.2 maximum_bitcast_fusion.4
  329.0 6.9 %copy.49 = bf16[1,128,2,1,32,128]{5,0,2,4,1,3:T(2,128)(2,1)} copy(bf16[1,128,2,1,32,128]{5,4,2,1,3,0:T(8,128)(2,1)S(1)} %maximum_bitcast_fusion.4) | data formatting | bytes 4194304 | tf_op jit(solution)/shard_map/stack | solution.py:29
  336.0 0.0 copy-done.1
  336.0 0.6 fusion.14
  336.6 6.9 %copy.48 = bf16[1,128,2,1,32,128]{5,0,2,4,1,3:T(2,128)(2,1)} copy(bf16[1,128,2,1,32,128]{5,4,2,1,3,0:T(8,128)(2,1)S(1)} %fusion.14) | data formatting | bytes 4194304 | tf_op jit(solution)/shard_map/stack | solution.py:29
  343.4 151.7 %all-gather.2.cloned.1.call-done = bf16[128,2,16,32,128]{4,3,1,0,2:T(8,128)(2,1)} async-done(((bf16[128,2,1,32,128]{4,3,1,0,2:T(8,128)(2,1)}), bf16[128,2,16,32,128]{4,3,1,0,2:T(8,128)(2,1)}) %all-gather.2.cloned.1.call-update) | async-done | bytes 33554448 | tf_op jit(solution)/shard_map/all_gather | solution.py:46
  495.1 34.7 %fusion.9 = f32[128,2,1,32,16]{4,1,3,0,2:T(2,128)} fusion(bf16[1,128,2,1,32,128]{5,0,2,4,1,3:T(2,128)(2,1)} %copy.49, bf16[1,128,2,1,32,128]{5,0,2,4,1,3:T(2,128)(2,1)} %copy.48, bf16[128,2,16,32,128]{4,3,1,0,2:T(8,128)(2,1)} %all-gather.2.cloned.1.call-done), kind=kOutput, calls=%fused_computation.24 | convolution fusion | flops 75497472 | bytes 38273024 | tf_op jit(solution)/shard_map/ofcsbt,fcrbt->fosbr/dot_general | solution.py:24
  529.8 5.9 %copy.51 = f32[128,2,1,32,16]{0,4,3,2,1:T(8,128)} copy(f32[128,2,1,32,16]{4,1,3,0,2:T(2,128)} %fusion.9) | data formatting | bytes 1048576 | tf_op jit(solution)/shard_map/ofcsbt,fcrbt->fosbr/transpose | solution.py:24
  (2 shorter events, 0.0 us)
Async XLA Ops:
  6.5 313.5 %reduce-scatter.5.cloned.1.call-start = ((), (), s32[]{:S(2)}) async-start(), calls=%async_computation.2 | async-start | bytes 12582912
  7.9 35.5 %copy-start.2 = (s32[1,128]{1,0:T(1,128)S(1)}, s32[1,128]{1,0:T(1,128)}, u32[]{:S(2)}) copy-start(s32[1,128]{1,0:T(1,128)} %param.6) | copy-start | bytes 1540
  217.9 277.2 %all-gather.2.cloned.1.call-start = ((), (), s32[]{:S(2)}) async-start(), calls=%async_computation.1 | async-start | bytes 35651584 | tf_op jit(solution)/shard_map/all_gather | solution.py:46
  323.0 2.0 copy-start
  326.9 9.1 %copy-start.1 = (f32[16,8,64,128]{3,2,1,0:T(8,128)S(1)}, f32[16,8,64,128]{3,2,1,0:T(8,128)}, u32[]{:S(2)}) copy-start(f32[16,8,64,128]{3,2,1,0:T(8,128)} %copy-done) | copy-start | bytes 12582916
Sparse Core Ops, SparseCore 0:
  218.0 102.0 reduce-scatter.4
  327.0 168.0 all-gather.1
where the time goes:
time: 552 us; the launch traced here: 543 us
  waiting for transfers between devices  246 us (45%)
  local copies, waits for them, and re-layouts  114 us (21%)
  matrix products  108 us (20%)
  other arithmetic  53.6 us (10%)
  between operations  14.6 us (3%)
  blocking collectives  6.72 us (1%)
    all_gather x1, waiting for transfers between devices, on_device(): lax.all_gather(beam_data, 'station', axis=2, tiled=True)  152 us
    unnamed x3, waiting for transfers between devices  94.2 us
    dot_general x4, matrix products, contract(): jnp.einsum('sabf,satf->fsbt', left, right, precision=lax.Precision.HIGHES...  73.4 us
    unnamed x11, local copies, waits for them, and re-layouts  63 us
    dot_general x1, matrix products, correlate(): jnp.einsum('ofcsbt,fcrbt->fosbr', stacked, arrived, preferred_element_typ...  34.7 us
    mul x2, other arithmetic, on_device(): masked = samples * usable[None, :, :, None, None]  23.7 us
    gather x1, local copies, waits for them, and re-layouts, on_device(): jnp.take(masked, subband_table, axis=4)  23.6 us
    another operation x2, local copies, waits for them, and re-layouts, with_swapped(): return jnp.stack([beam_data, swapped], axis=0)  13.8 us
  transfers between devices with their start and end apart: 2, of which 2 were waited for; matrix products, arithmetic and copies ran while one was open for 3% of the time, Pallas kernels for 0%

commit v1 on v0

--- a/solution.py
+++ b/solution.py
@@ -1,7 +1,17 @@
+import functools
 import jax
 import jax.numpy as jnp
 from jax import lax
 from jax.sharding import PartitionSpec as P
+
+
+def work_indices(s0, group_axis):
+    back = lax.all_gather(s0, axis_name=group_axis)
+    main = jnp.concatenate(back, axis=2)
+    return main
+
+
+press_body = functools.partial(work_indices, group_axis="station")
 
 
 def beamform(steer, signal):
@@ -43,7 +53,7 @@
     )
     beam_data = (beam_sum * gain_scale[None, None, :, None, None]).astype(jnp.bfloat16)
     stacked = with_swapped(beam_data)
-    return correlate(stacked, lax.all_gather(beam_data, "station", axis=2, tiled=True))
+    return correlate(stacked, press_body(beam_data))
 
 
 def solution(mesh):

time: 552 us -> 552 us (level)
    all_gather x0 -> x1, local copies, waits for them, and re-layouts: none -> 6.85 us  [work_indices(): back = lax.all_gather(s0, axis_name=group_axis)]
    another operation x2 -> x1, local copies, waits for them, and re-layouts: 13.8 us -> 6.94 us  [with_swapped(): return jnp.stack([beam_data, swapped], axis=0)]
where the time goes in v1:
time: 552 us; the launch traced here: 543 us
  waiting for transfers between devices  245 us (44%)
  local copies, waits for them, and re-layouts  114 us (21%)
  matrix products  108 us (20%)
  other arithmetic  54.7 us (10%)
  between operations  14.6 us (3%)
  blocking collectives  6.72 us (1%)
    all_gather x1, waiting for transfers between devices, work_indices(): back = lax.all_gather(s0, axis_name=group_axis)  151 us
    unnamed x3, waiting for transfers between devices  94.2 us
    dot_general x4, matrix products, contract(): jnp.einsum('sabf,satf->fsbt', left, right, precision=lax.Precision.HIGHES...  73.4 us
    unnamed x11, local copies, waits for them, and re-layouts  63 us
    dot_general x1, matrix products, correlate(): jnp.einsum('ofcsbt,fcrbt->fosbr', stacked, arrived, preferred_element_typ...  34.7 us
    mul x2, other arithmetic, on_device(): masked = samples * usable[None, :, :, None, None]  23.7 us
    gather x1, local copies, waits for them, and re-layouts, on_device(): jnp.take(masked, subband_table, axis=4)  23.6 us
    select_n x1, other arithmetic, on_device(): jnp.take(masked, subband_table, axis=4)  12.9 us
  transfers between devices with their start and end apart: 2, of which 2 were waited for; matrix products, arithmetic and copies ran while one was open for 3% of the time, Pallas kernels for 0%

profile of v1, /device:TPU:0, one launch (start us, length us, event | category | flops | bytes accessed | tf_op | source)
XLA Modules:
  0.0 543.0 jit_solution(9990091042379952151)
XLA Ops:
  6.5 0.0 reduce-scatter.5.cloned.1.call-start
  6.5 0.7 compare_select_fusion
  7.2 0.7 compare_and_fusion
  7.9 0.0 copy-start.2
  7.9 35.5 %copy.51 = f32[2,1,128,128,256]{3,2,0,4,1:T(8,128)} copy(f32[2,1,128,128,256]{4,3,2,1,0:T(8,128)} %param.4) | data formatting | bytes 67108864 | tf_op args[0]
  43.4 0.0 copy-done.2
  43.4 10.3 %copy.49 = f32[2,1,32,128,256]{3,2,0,4,1:T(8,128)} copy(f32[2,1,32,128,256]{4,3,2,1,0:T(8,128)} %param.5) | data formatting | bytes 16777216 | tf_op args[1]
  53.8 23.7 %multiply_bitcast_fusion = f32[2,128,128,256]{2,1,0,3:T(8,128)} fusion(f32[2,1,128,128,256]{3,2,0,4,1:T(8,128)} %copy.51, f32[128]{0:T(128)S(1)} %convert_bitcast_fusion), kind=kLoop, calls=%fused_computation.6 | loop fusion | flops 8388608 | bytes 67109376 | tf_op jit(solution)/shard_map/mul | solution.py:46
  77.4 23.6 %gather_fusion.1 = f32[256,2,128,128]{3,2,1,0:T(8,128)} fusion(f32[2,128,128,256]{2,1,0,3:T(8,128)} %multiply_bitcast_fusion, s32[1024]{0:T(1024)S(1)} %pad_clamp_fusion), kind=kCustom, calls=%fused_computation.1 | custom fusion | bytes 67109888 | tf_op jit(solution)/shard_map/jit(_take)/gather | solution.py:49
  101.0 7.7 %gather_fusion = f32[256,2,128,32]{2,3,1,0:T(8,128)} fusion(f32[2,128,32,256]{1,2,0,3:T(8,128)} %bitcast.93, s32[1024]{0:T(1024)S(1)} %pad_clamp_fusion), kind=kCustom, calls=%fused_computation | custom fusion | bytes 16778240 | tf_op jit(solution)/shard_map/jit(_take)/gather | solution.py:49
  108.7 12.9 %bitcast_select_fusion = f32[2,1,128,128,256]{3,2,4,1,0:T(8,128)S(1)} fusion(f32[256,2,128,128]{3,2,1,0:T(8,128)} %gather_fusion.1, pred[256]{0:T(512)(128)(4,1)S(1)} %compare_and_fusion), kind=kLoop, calls=%fused_computation.4 | loop fusion | flops 8388608 | bytes 67109120 | tf_op jit(solution)/shard_map/jit(_take)/select_n | solution.py:49
  121.6 6.0 %bitcast_select_fusion.1 = f32[2,1,128,32,256]{2,3,4,1,0:T(8,128)} fusion(f32[256,2,128,32]{2,3,1,0:T(8,128)} %gather_fusion, pred[256]{0:T(512)(128)(4,1)S(1)} %compare_and_fusion), kind=kLoop, calls=%fused_computation.15 | loop fusion | flops 2097152 | bytes 16777472 | tf_op jit(solution)/shard_map/jit(_take)/select_n | solution.py:49
  127.6 17.8 %fusion.4 = f32[256,32,128]{2,1,0:T(8,128)} fusion(f32[2,1,128,128,256]{3,2,4,1,0:T(8,128)S(1)} %bitcast_select_fusion, f32[2,1,128,32,256]{2,3,4,1,0:T(8,128)} %bitcast_select_fusion.1), kind=kOutput, calls=%fused_computation.10 | convolution fusion | flops 1610612736 | bytes 25165824 | tf_op jit(solution)/shard_map/sabf,satf->fsbt/dot_general | solution.py:20
  145.4 18.0 %fusion.3 = f32[256,32,128]{2,1,0:T(8,128)} fusion(f32[2,1,128,128,256]{3,2,4,1,0:T(8,128)S(1)} %bitcast_select_fusion, f32[2,1,128,32,256]{2,3,4,1,0:T(8,128)} %bitcast_select_fusion.1), kind=kOutput, calls=%fused_computation.9 | convolution fusion | flops 1610612736 | bytes 25165824 | tf_op jit(solution)/shard_map/sabf,satf->fsbt/dot_general | solution.py:20
  163.4 18.7 %subtract_bitcast_fusion = f32[256,1,1,32,128]{4,3,0,2,1:T(8,128)} fusion(f32[256,32,128]{2,1,0:T(8,128)} %fusion.4, f32[2,1,128,128,256]{3,2,4,1,0:T(8,128)S(1)} %bitcast_select_fusion, f32[2,1,128,32,256]{2,3,4,1,0:T(8,128)} %bitcast_select_fusion.1), kind=kOutput, calls=%fused_computation.24 | convolution fusion | flops 1611661312 | bytes 29360128 | tf_op jit(solution)/shard_map/sabf,satf->fsbt/dot_general | solution.py:20
  182.0 19.0 %add_bitcast_fusion = f32[256,1,1,32,128]{4,3,0,2,1:T(8,128)} fusion(f32[256,32,128]{2,1,0:T(8,128)} %fusion.3, f32[2,1,128,128,256]{3,2,4,1,0:T(8,128)S(1)} %bitcast_select_fusion, f32[2,1,128,32,256]{2,3,4,1,0:T(8,128)} %bitcast_select_fusion.1), kind=kOutput, calls=%fused_computation.23 | convolution fusion | flops 1611661312 | bytes 29360128 | tf_op jit(solution)/shard_map/sabf,satf->fsbt/dot_general | solution.py:20
  201.1 4.4 pad_maximum_fusion
  205.5 1.4 copy.60
  207.0 10.9 %copy.74 = f32[32,8,64,128]{3,1,2,0:T(8,128)} copy(f32[32,8,64,128]{3,2,1,0:T(8,128)S(1)} %bitcast.94) | data formatting | bytes 16777216
  217.8 0.0 reduce-scatter.5.cloned.1.call-update
  217.9 0.0 all-gather.3.cloned.1.call-start
  217.9 0.6 convert_reduce_fusion
  218.5 6.7 %psum.7 = f32[1]{0:T(128)} all-reduce(f32[1]{0:T(128)} %bitcast.14), channel_id=1, replica_groups=mesh['station'=16,'chan'=2] {'chan'}, use_global_device_ids=true, to_apply=%region_2.3 | all-reduce | flops 1 | bytes 8 | tf_op jit(solution)/shard_map/psum | solution.py:44
  225.9 94.1 %reduce-scatter.5.cloned.1.call-done = f32[128,8192]{1,0:T(8,128)} async-done(((f32[256,8192]{1,0:T(8,128)}), f32[128,8192]{1,0:T(8,128)}) %reduce-scatter.5.cloned.1.call-update) | async-done | bytes 4194320
  320.1 2.9 copy.64
  323.0 0.0 copy-start
  323.0 1.9 copy-done
  324.9 1.9 fusion.15
  326.9 0.0 all-gather.3.cloned.1.call-update
  326.9 2.8 fusion.9
  329.7 0.0 copy-start.1
  329.7 0.2 fusion.14
  329.9 0.2 maximum_bitcast_fusion.4
  330.1 6.9 %copy.57 = bf16[1,128,2,1,32,128]{5,0,2,4,1,3:T(2,128)(2,1)} copy(bf16[1,128,2,1,32,128]{5,4,2,1,3,0:T(8,128)(2,1)S(1)} %maximum_bitcast_fusion.4) | data formatting | bytes 4194304 | tf_op jit(solution)/shard_map/stack | solution.py:39
  337.1 0.0 copy-done.1
  337.1 0.6 fusion.16
  337.7 6.9 %copy.56 = bf16[1,128,2,1,32,128]{5,0,2,4,1,3:T(2,128)(2,1)} copy(bf16[1,128,2,1,32,128]{5,4,2,1,3,0:T(8,128)(2,1)S(1)} %fusion.16) | data formatting | bytes 4194304 | tf_op jit(solution)/shard_map/all_gather | solution.py:9
  344.5 150.6 %all-gather.3.cloned.1.call-done = bf16[2048,2,1,32,128]{4,3,2,1,0:T(8,128)(2,1)} async-done(((bf16[128,2,1,32,128]{4,3,2,1,0:T(8,128)(2,1)}), bf16[2048,2,1,32,128]{4,3,2,1,0:T(8,128)(2,1)}) %all-gather.3.cloned.1.call-update) | async-done | bytes 33554448 | tf_op jit(solution)/shard_map/all_gather | solution.py:9
  495.1 34.7 %fusion.10 = f32[128,2,1,32,16]{4,1,3,0,2:T(2,128)} fusion(bf16[1,128,2,1,32,128]{5,0,2,4,1,3:T(2,128)(2,1)} %copy.57, bf16[1,128,2,1,32,128]{5,0,2,4,1,3:T(2,128)(2,1)} %copy.56, bf16[16,128,2,1,32,128]{5,4,2,1,0,3:T(8,128)(2,1)} %bitcast.96), kind=kOutput, calls=%fused_computation.25 | convolution fusion | flops 75497472 | bytes 38273024 | tf_op jit(solution)/shard_map/ofcsbt,fcrbt->fosbr/dot_general | solution.py:34
  529.8 5.9 %copy.58 = f32[128,2,1,32,16]{0,4,3,2,1:T(8,128)} copy(f32[128,2,1,32,16]{4,1,3,0,2:T(2,128)} %fusion.10) | data formatting | bytes 1048576 | tf_op jit(solution)/shard_map/ofcsbt,fcrbt->fosbr/transpose | solution.py:34
  (2 shorter events, 0.0 us)
Async XLA Ops:
  6.5 313.5 %reduce-scatter.5.cloned.1.call-start = ((), (), s32[]{:S(2)}) async-start(), calls=%async_computation.2 | async-start | bytes 12582912
  7.9 35.5 %copy-start.2 = (s32[1,128]{1,0:T(1,128)S(1)}, s32[1,128]{1,0:T(1,128)}, u32[]{:S(2)}) copy-start(s32[1,128]{1,0:T(1,128)} %param.6) | copy-start | bytes 1540
  217.9 277.2 %all-gather.3.cloned.1.call-start = ((), (), s32[]{:S(2)}) async-start(), calls=%async_computation.1 | async-start | bytes 35651584 | tf_op jit(solution)/shard_map/all_gather | solution.py:9
  323.0 2.0 copy-start
  329.7 7.4 %copy-start.1 = (f32[16,8,64,128]{3,2,1,0:T(8,128)S(1)}, f32[16,8,64,128]{3,2,1,0:T(8,128)}, u32[]{:S(2)}) copy-start(f32[16,8,64,128]{3,2,1,0:T(8,128)} %copy-done) | copy-start | bytes 12582916
Sparse Core Ops, SparseCore 0:
  218.0 102.0 reduce-scatter.4
  327.0 168.0 all-gather.2
